TPU v7x, 32 devices: a whole 2x2x4 slice. The times are simulated.
32 devices in a mesh: seq: 16 (over z, y, core), ch: 2 (over x).
Axes of the slice: x: 2, y: 2, z: 4, core: 2. Of those that a mesh axis runs over, the one named last changes fastest.
Arguments:
- query_gate: bfloat16 [2, 2048, 2048], P('ch', 'seq'), may hold values from -6 to 6
- key_input: bfloat16 [2, 2048, 2048], P('ch', 'seq'), may hold values from -6 to 6
- value_input: bfloat16 [2, 2048, 2048], P('ch', 'seq'), may hold values from -6 to 6
- grad_output: bfloat16 [2, 2048, 2048], P('ch', 'seq'), may hold values from -6 to 6
- filter_raw: bfloat16 [2048, 2048], P('seq'), may hold values from -6 to 6
- skip_gain: float32 [2048], replicated, may hold values from 0.5 to 1.5
Outputs:
- grad_query: bfloat16 [2, 2048, 2048], P('ch', 'seq')
- grad_key: bfloat16 [2, 2048, 2048], P('ch', 'seq')
- grad_value: bfloat16 [2, 2048, 2048], P('ch', 'seq')
- grad_filter: float32 [2048, 2048], P('seq', 'ch')
All inputs are finite; a program needn't handle non-finite values.
Results may differ from a plain program's by a relative error of at most 0.001.
Values sent between devices are 32-bit elements; how exact they have to be, the bound alone decides.
A program may use at most 128 MiB of HBM per device.

v0:
```python
import math

import numpy as np

import jax
import jax.numpy as jnp
from jax import lax
from jax.experimental import pallas as pl
from jax.experimental.pallas import tpu as pltpu
from jax.sharding import PartitionSpec as P


def angle_table(row_index, col_index, modulus):
    turn_count = row_index[:, None] * col_index[None, :] % modulus
    angles = turn_count.astype(jnp.float32) * (2.0 * math.pi / modulus)
    return (jnp.cos(angles), jnp.sin(angles))


def contract(pattern, table, operand):
    return jnp.einsum(
        pattern, table, operand, precision=lax.Precision.HIGHEST, preferred_element_type=jnp.float32
    )


def rotate(pattern, cos_table, sin_table, sense_sign, real_part, imag_part, want_imag):
    if imag_part is None:
        cos_term = contract(pattern, cos_table, real_part)
        return (cos_term, sense_sign * contract(pattern, sin_table, real_part))
    real_out = contract(pattern, cos_table, real_part) - sense_sign * contract(
        pattern, sin_table, imag_part
    )
    if not want_imag:
        return (real_out, None)
    imag_out = contract(pattern, cos_table, imag_part) + sense_sign * contract(
        pattern, sin_table, real_part
    )
    return (real_out, imag_out)


def twist(cos_table, sin_table, sense_sign, real_part, imag_part):
    return (
        real_part * cos_table - sense_sign * imag_part * sin_table,
        imag_part * cos_table + sense_sign * real_part * sin_table,
    )


def spectral_terms(z_real, z_imag, g_real, g_imag, h_real, h_imag):
    conv_real = z_real * h_real - z_imag * h_imag
    conv_imag = z_real * h_imag + z_imag * h_real
    back_real = h_real * g_real + h_imag * g_imag
    back_imag = h_real * g_imag - h_imag * g_real
    corr_real = z_real * g_real + z_imag * g_imag
    corr_imag = z_real * g_imag - z_imag * g_real
    return (conv_real - back_imag, conv_imag + back_real, corr_real, corr_imag)


def shards(query_gate, key_input, value_input, grad_output, filter_raw, skip_gain):
    seq_count = lax.axis_size("seq")
    key_f = key_input[0].astype(jnp.float32)
    value_f = value_input[0].astype(jnp.float32)
    out_f = grad_output[0].astype(jnp.float32)
    mixed = key_f * value_f
    gated = out_f * query_gate[0].astype(jnp.float32)
    tokens, channels = mixed.shape
    seq_length = tokens * seq_count
    full_length = 2 * seq_length
    inverse_scale = 1.0 / full_length
    filter_taps = filter_raw.astype(jnp.float32) * seq_length ** (-0.5)
    freq_one = jnp.arange(2 * seq_count, dtype=jnp.int32)
    block_index = jnp.arange(seq_count, dtype=jnp.int32)
    offset_index = jnp.arange(tokens, dtype=jnp.int32)
    cos_one, sin_one = angle_table(freq_one, block_index, 2 * seq_count)
    cos_inv, sin_inv = angle_table(block_index, freq_one, 2 * seq_count)
    cos_two, sin_two = angle_table(offset_index, offset_index, tokens)
    local_width = channels // seq_count
    arrived = (
        lax.all_to_all(mixed.T, "seq", split_axis=0, concat_axis=1, tiled=True),
        lax.all_to_all(gated.T, "seq", split_axis=0, concat_axis=1, tiled=True),
        lax.all_to_all(filter_taps.T, "seq", split_axis=0, concat_axis=1, tiled=True),
    )
    cos_tw, sin_tw = angle_table(freq_one, offset_index, full_length)
    spectra = []
    for line_data in arrived:
        lines = line_data.reshape(local_width, seq_count, tokens)
        real_part, imag_part = rotate("kn,cnm->ckm", cos_one, sin_one, -1.0, lines, None, True)
        real_part, imag_part = twist(cos_tw, sin_tw, -1.0, real_part, imag_part)
        spectra.append(rotate("jm,ckm->ckj", cos_two, sin_two, -1.0, real_part, imag_part, True))
    packed_real, packed_imag, corr_real, corr_imag = spectral_terms(
        spectra[0][0], spectra[0][1], spectra[1][0], spectra[1][1], spectra[2][0], spectra[2][1]
    )
    pr_mid, pi_mid = rotate("mj,ckj->ckm", cos_two, sin_two, 1.0, packed_real, packed_imag, True)
    pr_mid, pi_mid = twist(cos_tw, sin_tw, 1.0, pr_mid, pi_mid)
    cr_mid, ci_mid = rotate("mj,ckj->ckm", cos_two, sin_two, 1.0, corr_real, corr_imag, True)
    cr_mid, ci_mid = twist(cos_tw, sin_tw, 1.0, cr_mid, ci_mid)
    conv_lines, back_lines = rotate("nk,ckm->cnm", cos_inv, sin_inv, 1.0, pr_mid, pi_mid, True)
    corr_lines = rotate("nk,ckm->cnm", cos_inv, sin_inv, 1.0, cr_mid, ci_mid, False)[0]
    conv_lines = (conv_lines * inverse_scale).reshape(local_width, seq_length)
    back_lines = (back_lines * inverse_scale).reshape(local_width, seq_length)
    corr_lines = (corr_lines * inverse_scale).reshape(local_width, seq_length)
    returned = (
        lax.all_to_all(conv_lines, "seq", split_axis=1, concat_axis=0, tiled=True),
        lax.all_to_all(back_lines, "seq", split_axis=1, concat_axis=0, tiled=True),
        lax.all_to_all(corr_lines, "seq", split_axis=1, concat_axis=0, tiled=True),
    )
    conv_time = returned[0].T
    back_time = returned[1].T
    corr_time = returned[2].T
    conv_full = conv_time + skip_gain * mixed
    back_full = back_time + skip_gain * gated
    grad_query = (out_f * conv_full).astype(jnp.bfloat16)[None]
    grad_key = (back_full * value_f).astype(jnp.bfloat16)[None]
    grad_value = (back_full * key_f).astype(jnp.bfloat16)[None]
    grad_filter = lax.psum_scatter(
        corr_time * seq_length ** (-0.5), "ch", scatter_dimension=1, tiled=True
    )
    return (grad_query, grad_key, grad_value, grad_filter)


LANES = 128
VMEM_LIMIT = 60 * 1024 * 1024


def times_root(pair, turn, size):
    real, imag = pair
    turn %= size
    if turn == 0:
        return pair
    if 4 * turn == size:
        return (-imag, real)
    if 2 * turn == size:
        return (-real, -imag)
    if 4 * turn == 3 * size:
        return (imag, -real)
    cosine = math.cos(2.0 * math.pi * turn / size)
    sine = math.sin(2.0 * math.pi * turn / size)
    return (real * cosine - imag * sine, real * sine + imag * cosine)


def complex_dft(values, sense):
    size = len(values)
    if size == 1:
        return values
    even = complex_dft(values[0::2], sense)
    odd = complex_dft(values[1::2], sense)
    low, high = [], []
    for k in range(size // 2):
        er, ei = even[k]
        tr, ti = times_root(odd[k], sense * k, size)
        low.append((er + tr, ei + ti))
        high.append((er - tr, ei - ti))
    return low + high


def half_spectrum(values, size):
    if size == 2:
        return [(values[0] + values[1], None), (values[0] - values[1], None)]
    half, quarter = size // 2, size // 4
    if len(values) == half:
        total, difference = values, values
    else:
        total = [values[n] + values[n + half] for n in range(half)]
        difference = [values[n] - values[n + half] for n in range(half)]
    out = [None] * (half + 1)
    out[0::2] = half_spectrum(total, half)
    turned = [times_root((difference[n], -difference[n + quarter]), -n, size) for n in range(quarter)]
    for index, (real, imag) in enumerate(complex_dft(turned, -1)):
        k = 1 + 4 * index
        if k <= half:
            out[k] = (real, imag)
        else:
            out[size - k] = (real, -imag)
    return out


def real_from_half(terms, size, first_half):
    if size == 2:
        return [terms[0][0] + terms[1][0], terms[0][0] - terms[1][0]]
    half, quarter = size // 2, size // 4
    even = real_from_half(terms[0::2], half, False)
    chosen = []
    for index in range(quarter):
        k = 1 + 4 * index
        if k <= half:
            chosen.append(terms[k])
        else:
            real, imag = terms[size - k]
            chosen.append((real, -imag))
    turned = [times_root(pair, n, size) for n, pair in enumerate(complex_dft(chosen, 1))]
    odd = [pair[0] for pair in turned] + [-pair[1] for pair in turned]
    out = [even[n] + odd[n] for n in range(half)]
    if first_half:
        return out
    return out + [even[n] - odd[n] for n in range(half)]


def split_bf16(value):
    high = value.astype(jnp.bfloat16)
    return high, (value - high.astype(jnp.float32)).astype(jnp.bfloat16)


def three_dot(table_high, table_low, value):
    high, low = split_bf16(value)
    dot = lambda a, b: jnp.dot(a, b, preferred_element_type=jnp.float32)
    return dot(table_high, high) + (dot(table_high, low) + dot(table_low, high))


def fft_kernel(seq_count, tokens, pair_ref, taps_ref, fwd_ref, inv_ref, tw_ref, out_pair_ref, out_corr_ref, spec_ref, taps_scr, corr_scr):
    half_lanes = LANES // 2
    half_tokens = tokens // 2
    size = 2 * seq_count

    def spread_taps(block, carry):
        packed = taps_ref[block]
        rolled = pltpu.roll(packed, half_lanes, 1)
        lane = lax.broadcasted_iota(jnp.int32, packed.shape, 1)
        left = lane < half_lanes
        taps_scr[block, :half_tokens, :] = jnp.where(left, packed, rolled)
        taps_scr[block, half_tokens:, :] = jnp.where(left, rolled, packed)
        return carry

    lax.fori_loop(0, seq_count, spread_taps, 0)

    def analyse(chunk, carry):
        rows = pl.ds(pl.multiple_of(chunk * 8, 8), 8)
        for signal in range(3):
            lanes = slice(signal * LANES, (signal + 1) * LANES)
            if signal < 2:
                values = [pair_ref[signal, n, rows, :] for n in range(seq_count)]
            else:
                values = [taps_scr[n, rows, :] for n in range(seq_count)]
            for k, (real, imag) in enumerate(half_spectrum(values, size)):
                spec_ref[k, 0, rows, lanes] = real
                spec_ref[k, 1, rows, lanes] = jnp.zeros_like(real) if imag is None else imag
        return carry

    lax.fori_loop(0, tokens // 8, analyse, 0)

    fwd_high, fwd_low = fwd_ref[0], fwd_ref[1]
    inv_high, inv_low = inv_ref[0], inv_ref[1]

    def middle(k, carry):
        cosine = jnp.concatenate([tw_ref[k, 0]] * 3, axis=1)
        sine = jnp.concatenate([tw_ref[k, 1]] * 3, axis=1)
        real, imag = spec_ref[k, 0], spec_ref[k, 1]
        turned = jnp.concatenate([real * cosine + imag * sine, imag * cosine - real * sine], axis=0)
        spectra = three_dot(fwd_high, fwd_low, turned)
        sr, si = spectra[:tokens], spectra[tokens:]
        a_r, b_r, h_r = (sr[:, i * LANES:(i + 1) * LANES] for i in range(3))
        a_i, b_i, h_i = (si[:, i * LANES:(i + 1) * LANES] for i in range(3))
        lane = lax.broadcasted_iota(jnp.int32, h_i.shape, 1)
        h_i = jnp.where(lane < half_lanes, h_i, -h_i)
        swap = lambda v: pltpu.roll(v, half_lanes, 1)
        ga_r, ga_i, gb_r, gb_i = swap(a_r), swap(a_i), swap(b_r), swap(b_i)
        prod_r = jnp.concatenate([
            a_r * h_r - a_i * h_i,
            b_r * h_r - b_i * h_i,
            a_r * ga_r + a_i * ga_i + b_r * gb_r + b_i * gb_i], axis=1)
        prod_i = jnp.concatenate([
            a_r * h_i + a_i * h_r,
            b_r * h_i + b_i * h_r,
            a_r * ga_i - a_i * ga_r + b_r * gb_i - b_i * gb_r], axis=1)
        back = three_dot(inv_high, inv_low, jnp.concatenate([prod_r, prod_i], axis=0))
        br, bi = back[:tokens], back[tokens:]
        weight = jnp.where((k == 0) | (k == seq_count), 0.5 / (seq_count * tokens), 1.0 / (seq_count * tokens))
        cosine, sine = cosine * weight, sine * weight
        spec_ref[k, 0] = br * cosine - bi * sine
        spec_ref[k, 1] = bi * cosine + br * sine
        return carry

    lax.fori_loop(0, seq_count + 1, middle, 0)

    def synthesise(chunk, carry):
        rows = pl.ds(pl.multiple_of(chunk * 8, 8), 8)
        for signal in range(3):
            lanes = slice(signal * LANES, (signal + 1) * LANES)
            terms = [(spec_ref[k, 0, rows, lanes], spec_ref[k, 1, rows, lanes]) for k in range(seq_count + 1)]
            for n, value in enumerate(real_from_half(terms, size, True)):
                if signal < 2:
                    out_pair_ref[signal, n, rows, :] = value
                else:
                    corr_scr[n, rows, :] = value
        return carry

    lax.fori_loop(0, tokens // 8, synthesise, 0)
    corr_scale = (seq_count * tokens) ** -0.5

    def gather_corr(block, carry):
        top = corr_scr[block, :half_tokens, :]
        bottom = pltpu.roll(corr_scr[block, half_tokens:, :], half_lanes, 1)
        lane = lax.broadcasted_iota(jnp.int32, top.shape, 1)
        out_corr_ref[block] = jnp.where(lane < half_lanes, top, bottom) * corr_scale
        return carry

    lax.fori_loop(0, seq_count, gather_corr, 0)


def left_mask(shape):
    return lax.broadcasted_iota(jnp.int32, shape, 1) < LANES // 2


def gate_kernel(query_ref, key_ref, value_ref, out_ref, pair_ref):
    mixed = key_ref[...].astype(jnp.float32) * value_ref[...].astype(jnp.float32)
    gated = out_ref[...].astype(jnp.float32) * query_ref[...].astype(jnp.float32)
    left = left_mask(mixed.shape)
    pair_ref[0] = jnp.where(left, mixed, pltpu.roll(gated, LANES // 2, 1))
    pair_ref[1] = jnp.where(left, pltpu.roll(mixed, LANES // 2, 1), gated)


def finish_kernel(pair_ref, query_ref, key_ref, value_ref, out_ref, skip_ref, gq_ref, gk_ref, gv_ref):
    query_f = query_ref[...].astype(jnp.float32)
    key_f = key_ref[...].astype(jnp.float32)
    value_f = value_ref[...].astype(jnp.float32)
    out_f = out_ref[...].astype(jnp.float32)
    first, second = pair_ref[0], pair_ref[1]
    left = left_mask(first.shape)
    skip = skip_ref[...]
    conv = jnp.where(left, first, pltpu.roll(second, LANES // 2, 1)) + skip * (key_f * value_f)
    back = jnp.where(left, pltpu.roll(first, LANES // 2, 1), second) + skip * (out_f * query_f)
    gq_ref[...] = (out_f * conv).astype(jnp.bfloat16)
    gk_ref[...] = (back * value_f).astype(jnp.bfloat16)
    gv_ref[...] = (back * key_f).astype(jnp.bfloat16)


def tables(seq_count, tokens):
    index = np.arange(tokens)
    angle = 2.0 * np.pi / tokens * (index[:, None] * index[None, :] % tokens)
    cosine, sine = np.cos(angle), np.sin(angle)
    forward = np.block([[cosine, sine], [-sine, cosine]]).astype(np.float32)
    inverse = np.block([[cosine, -sine], [sine, cosine]]).astype(np.float32)

    def pieces(table):
        table = jnp.asarray(table)
        return jnp.stack(split_bf16(table))

    turn = 2.0 * np.pi / (2 * seq_count * tokens) * (np.arange(seq_count + 1)[:, None] * index[None, :])
    twiddle = np.stack([np.cos(turn), np.sin(turn)], axis=1).astype(np.float32)
    twiddle = jnp.broadcast_to(jnp.asarray(twiddle)[..., None], twiddle.shape + (LANES,))
    return pieces(forward), pieces(inverse), twiddle


def fast_shards(query_gate, key_input, value_input, grad_output, filter_raw, skip_gain):
    seq_count, ch_count = lax.axis_size("seq"), lax.axis_size("ch")
    owners = seq_count * ch_count
    _, tokens, channels = key_input.shape
    length = seq_count * tokens
    width = channels // owners
    groups = channels // LANES
    block = pl.BlockSpec((None, tokens, LANES), lambda i: (0, 0, i))
    pair_block = pl.BlockSpec((2, tokens, LANES), lambda i: (i, 0, 0))
    params = pltpu.CompilerParams(vmem_limit_bytes=VMEM_LIMIT)
    pair = pl.pallas_call(
        gate_kernel,
        grid=(groups,),
        in_specs=[block] * 4,
        out_specs=pair_block,
        out_shape=jax.ShapeDtypeStruct((owners, tokens, LANES), jnp.float32),
        name="gate",
    )(query_gate, key_input, value_input, grad_output)
    mine = lax.axis_index("ch") * (channels // ch_count)
    taps = lax.dynamic_slice_in_dim(filter_raw, mine, channels // ch_count, axis=1)
    taps = taps.astype(jnp.float32) * length ** (-0.5)
    taps = taps.reshape(2, tokens // 2, seq_count, width).transpose(2, 1, 0, 3)
    taps = taps.reshape(seq_count, tokens // 2, LANES)
    pair = lax.all_to_all(pair, ("ch", "seq"), split_axis=0, concat_axis=0, tiled=True)
    taps = lax.all_to_all(taps, "seq", split_axis=0, concat_axis=0, tiled=True)
    pair, corr = pl.pallas_call(
        lambda *refs: fft_kernel(seq_count, tokens, *refs),
        out_shape=(
            jax.ShapeDtypeStruct((ch_count, seq_count, tokens, LANES), jnp.float32),
            jax.ShapeDtypeStruct((seq_count, tokens // 2, LANES), jnp.float32),
        ),
        scratch_shapes=[
            pltpu.VMEM((seq_count + 1, 2, tokens, 3 * LANES), jnp.float32),
            pltpu.VMEM((seq_count, tokens, LANES), jnp.float32),
            pltpu.VMEM((seq_count, tokens, LANES), jnp.float32),
        ],
        compiler_params=params,
        name="convolve",
    )(pair.reshape(ch_count, seq_count, tokens, LANES), taps, *tables(seq_count, tokens))
    pair = lax.all_to_all(pair.reshape(owners, tokens, LANES), ("ch", "seq"), split_axis=0, concat_axis=0, tiled=True)
    corr = lax.all_to_all(corr, "seq", split_axis=0, concat_axis=0, tiled=True)
    grads = pl.pallas_call(
        finish_kernel,
        grid=(groups,),
        in_specs=[pair_block] + [block] * 4 + [pl.BlockSpec((1, LANES), lambda i: (0, i))],
        out_specs=[block] * 3,
        out_shape=[jax.ShapeDtypeStruct(key_input.shape, jnp.bfloat16)] * 3,
        name="finish",
    )(pair, query_gate, key_input, value_input, grad_output, skip_gain[None])
    corr = corr.reshape(seq_count, tokens // 2, 2, width).transpose(2, 1, 0, 3)
    return (*grads, corr.reshape(tokens, seq_count * width))


def solution(mesh):
    in_specs = (
        P("ch", "seq", None),
        P("ch", "seq", None),
        P("ch", "seq", None),
        P("ch", "seq", None),
        P("seq", None),
        P(),
    )
    out_specs = (P("ch", "seq", None), P("ch", "seq", None), P("ch", "seq", None), P("seq", "ch"))

    def body(*arrays):
        seq_count, ch_count = mesh.shape["seq"], mesh.shape["ch"]
        _, tokens, channels = arrays[0].shape
        fits = ch_count == 2 and tokens == LANES and channels == seq_count * LANES and seq_count <= 32
        return (fast_shards if fits else shards)(*arrays)

    return jax.shard_map(body, mesh=mesh, in_specs=in_specs, out_specs=out_specs, check_vma=False)
```

profile of v0, /device:TPU:0, one launch (start us, length us, event | category | flops | bytes accessed | tf_op | source)
XLA Modules:
  0.0 188.3 jit_solution(15909129051622946750)
XLA Ops:
  0.6 1.0 convert_multiply_fusion
  1.6 0.3 reshape.28
  1.9 0.8 copy.16
  2.7 1.4 reshape.29
  4.1 7.4 %all-to-all-start.1 = ((f32[16,64,128]{2,1,0:T(8,128)}), f32[16,64,128]{2,1,0:T(8,128)S(1)}, u32[]{:S(2)}, u32[]{:S(2)}) async-start(f32[16,64,128]{2,1,0:T(8,128)} %reshape.29), calls=%async_computation.1 | async-start | bytes 1048576 | tf_op jit(solution)/shard_map/all_to_all | solution.py:365
  11.6 9.5 %gate.1 = f32[32,128,128]{2,1,0:T(8,128)} custom-call(bf16[1,128,2048]{2,1,0:T(8,128)(2,1)} %query_ref.3, bf16[1,128,2048]{2,1,0:T(8,128)(2,1)} %key_ref.3, bf16[1,128,2048]{2,1,0:T(8,128)(2,1)} %value_ref.3, bf16[1,128,2048]{2,1,0:T(8,128)(2,1)} %out_ref.3), custom_call_target="tpu_custom_call" | custom-call | tf_op jit(solution)/shard_map/gate/pallas_call | solution.py:351
  21.0 0.0 copy-start.2
  21.0 4.8 %all-to-all-done.1.refs_1_ = f32[16,64,128]{2,1,0:T(8,128)S(1)} async-done(((f32[16,64,128]{2,1,0:T(8,128)}), f32[16,64,128]{2,1,0:T(8,128)S(1)}, u32[]{:S(2)}, u32[]{:S(2)}) %all-to-all-start.1) | async-done | bytes 524320 | tf_op jit(solution)/shard_map/all_to_all | solution.py:365
  25.8 0.0 copy-start.1
  25.8 53.8 %all_to_all.20 = f32[32,128,128]{2,1,0:T(8,128)} all-to-all(f32[32,128,128]{2,1,0:T(8,128)} %gate.1), channel_id=1, replica_groups=mesh['seq'=16,'ch'=2] {'ch','seq'}, dimensions={0} | all-to-all | bytes 4194304 | tf_op jit(solution)/shard_map/all_to_all | solution.py:364
  79.6 0.0 copy-done.1
  79.6 0.0 copy-done.2
  79.6 2.0 %broadcast_in_dim.4.refs_4_ = f32[17,2,128,128]{3,2,1,0:T(8,128)} broadcast(f32[17,2,128]{2,1,0:T(2,128)S(1)} %copy-done.2), dimensions={0,1,2} | broadcast | bytes 2245632 | tf_op jit(solution)/shard_map/broadcast_in_dim | solution.py:337
  81.7 23.1 %convolve.1 = (f32[2,16,128,128]{3,2,1,0:T(8,128)}, f32[16,64,128]{2,1,0:T(8,128)}) custom-call(f32[2,16,128,128]{3,2,1,0:T(8,128)} %bitcast.9, f32[16,64,128]{2,1,0:T(8,128)} %copy-done.1, bf16[2,256,256]{2,1,0:T(8,128)(2,1)} %constant.31.refs_2_, bf16[2,256,256]{2,1,0:T(8,128)(2,1)} %constant.38.refs_3_, f32[17,2,128,128]{3,2,1,0:T(8,128)} %broadcast_in_dim.4.refs_4_), custom_call_target="tpu_custom_call" | custom-call | tf_op jit(solution)/shard_map/convolve/pallas_call | solution.py:366
  104.7 18.5 %all_to_all.21 = f32[16,64,128]{2,1,0:T(8,128)} all-to-all(f32[16,64,128]{2,1,0:T(8,128)} %get-tuple-element.13), channel_id=1, replica_groups=mesh['seq'=16,'ch'=2] {'seq'}, dimensions={0} | all-to-all | bytes 1048576 | tf_op jit(solution)/shard_map/all_to_all | solution.py:381
  123.2 3.4 %all-to-all-start.2 = ((f32[32,128,128]{2,1,0:T(8,128)}), f32[32,128,128]{2,1,0:T(8,128)S(1)}, u32[]{:S(2)}, u32[]{:S(2)}) async-start(f32[32,128,128]{2,1,0:T(8,128)} %bitcast.12), calls=%async_computation.2 | async-start | bytes 4194304 | tf_op jit(solution)/shard_map/all_to_all | solution.py:380
  126.7 1.7 reshape.31
  128.3 1.6 copy.14
  129.9 2.3 %reshape.32 = f32[128,1024]{1,0:T(8,128)} reshape(f32[2,64,16,64]{3,2,1,0:T(8,128)} %copy.14) | data formatting | bytes 1048576 | tf_op jit(solution)/shard_map/reshape | solution.py:391
  132.2 44.5 %all-to-all-done.2.pair_ref = f32[32,128,128]{2,1,0:T(8,128)S(1)} async-done(((f32[32,128,128]{2,1,0:T(8,128)}), f32[32,128,128]{2,1,0:T(8,128)S(1)}, u32[]{:S(2)}, u32[]{:S(2)}) %all-to-all-start.2) | async-done | bytes 2097184 | tf_op jit(solution)/shard_map/all_to_all | solution.py:380
  176.7 0.0 copy-start
  176.7 1.3 copy-done
  178.1 10.2 %finish.1 = (bf16[1,128,2048]{2,1,0:T(8,128)(2,1)}, bf16[1,128,2048]{2,1,0:T(8,128)(2,1)}, bf16[1,128,2048]{2,1,0:T(8,128)(2,1)}) custom-call(f32[32,128,128]{2,1,0:T(8,128)} %copy-done, bf16[1,128,2048]{2,1,0:T(8,128)(2,1)} %query_ref.3, bf16[1,128,2048]{2,1,0:T(8,128)(2,1)} %key_ref.3, bf16[1,128,2048]{2,1,0:T(8,128)(2,1)} %value_ref.3, ...), custom_call_target="tpu_custom_call" | custom-call | tf_op jit(solution)/shard_map/finish/pallas_call | solution.py:382
Async XLA Ops:
  4.1 21.7 %all-to-all-start.1 = ((f32[16,64,128]{2,1,0:T(8,128)}), f32[16,64,128]{2,1,0:T(8,128)S(1)}, u32[]{:S(2)}, u32[]{:S(2)}) async-start(f32[16,64,128]{2,1,0:T(8,128)} %reshape.29), calls=%async_computation.1 | async-start | bytes 1048576 | tf_op jit(solution)/shard_map/all_to_all | solution.py:365
  21.0 58.6 %copy-start.2 = (f32[17,2,128]{2,1,0:T(2,128)S(1)}, f32[17,2,128]{2,1,0:T(2,128)}, u32[]{:S(2)}) copy-start(f32[17,2,128]{2,1,0:T(2,128)} %constant.18.clone) | copy-start | bytes 52228
  25.8 53.8 %copy-start.1 = (f32[16,64,128]{2,1,0:T(8,128)}, f32[16,64,128]{2,1,0:T(8,128)S(1)}, u32[]{:S(2)}) copy-start(f32[16,64,128]{2,1,0:T(8,128)S(1)} %all-to-all-done.1.refs_1_) | copy-start | bytes 1572868
  123.2 53.5 %all-to-all-start.2 = ((f32[32,128,128]{2,1,0:T(8,128)}), f32[32,128,128]{2,1,0:T(8,128)S(1)}, u32[]{:S(2)}, u32[]{:S(2)}) async-start(f32[32,128,128]{2,1,0:T(8,128)} %bitcast.12), calls=%async_computation.2 | async-start | bytes 4194304 | tf_op jit(solution)/shard_map/all_to_all | solution.py:380
  176.7 1.3 copy-start
where the time goes:
time: 190 us; the launch traced here: 188 us
  blocking collectives  72.3 us (38%)
  waiting for transfers between devices  49.3 us (26%)
  Pallas kernels  42.8 us (23%)
  local copies, waits for them, and re-layouts  11.4 us (6%)
  starting transfers between devices  10.8 us (6%)
    all_to_all x1, blocking collectives, fast_shards(): lax.all_to_all(pair, ('ch', 'seq'), split_axis=0, concat_axis=0, tiled=True)  53.8 us
    all_to_all x1, waiting for transfers between devices, fast_shards(): lax.all_to_all(pair.reshape(owners, tokens, LANES), ('ch', 'seq'), split_...  44.5 us
    pallas_call x1, Pallas kernels, fast_shards(): pl.pallas_call(lambda *refs: fft_kernel(seq_count, tokens, *refs), out_sh...  23.1 us
    all_to_all x1, blocking collectives, fast_shards(): corr = lax.all_to_all(corr, 'seq', split_axis=0, concat_axis=0, tiled=True)  18.5 us
    pallas_call x1, Pallas kernels, fast_shards(): pl.pallas_call(finish_kernel, grid=(groups,), in_specs=[pair_block] + [bl...  10.2 us
    pallas_call x1, Pallas kernels, fast_shards(): pl.pallas_call(gate_kernel, grid=(groups,), in_specs=[block] * 4, out_spe...  9.48 us
    all_to_all x1, starting transfers between devices, fast_shards(): taps = lax.all_to_all(taps, 'seq', split_axis=0, concat_axis=0, tiled=True)  7.41 us
    all_to_all x1, waiting for transfers between devices, fast_shards(): taps = lax.all_to_all(taps, 'seq', split_axis=0, concat_axis=0, tiled=True)  4.79 us
  transfers between devices with their start and end apart: 2, of which 2 were waited for; matrix products, arithmetic and copies ran while one was open for 3% of the time, Pallas kernels for 5%

commit v1 on v0

--- a/solution.py
+++ b/solution.py
@@ -204,18 +204,19 @@
     return dot(table_high, high) + (dot(table_high, low) + dot(table_low, high))
 
 
-def fft_kernel(seq_count, tokens, pair_ref, taps_ref, fwd_ref, inv_ref, tw_ref, out_pair_ref, out_corr_ref, spec_ref, taps_scr, corr_scr):
+def fft_kernel(seq_count, tokens, pair_ref, fwd_ref, inv_ref, tw_ref, out_pair_ref, out_corr_ref, spec_ref, taps_scr, corr_scr):
     half_lanes = LANES // 2
     half_tokens = tokens // 2
     size = 2 * seq_count
 
     def spread_taps(block, carry):
-        packed = taps_ref[block]
-        rolled = pltpu.roll(packed, half_lanes, 1)
-        lane = lax.broadcasted_iota(jnp.int32, packed.shape, 1)
-        left = lane < half_lanes
-        taps_scr[block, :half_tokens, :] = jnp.where(left, packed, rolled)
-        taps_scr[block, half_tokens:, :] = jnp.where(left, rolled, packed)
+        for part in range(2):
+            packed = pair_ref[part, block, tokens:, :]
+            rolled = pltpu.roll(packed, half_lanes, 1)
+            left = left_mask(packed.shape)
+            start, quarter = part * half_tokens, half_tokens // 2
+            taps_scr[block, start:start + quarter, :] = jnp.where(left, packed, rolled)
+            taps_scr[block, start + quarter:start + half_tokens, :] = jnp.where(left, rolled, packed)
         return carry
 
     lax.fori_loop(0, seq_count, spread_taps, 0)
@@ -298,27 +299,129 @@
     return lax.broadcasted_iota(jnp.int32, shape, 1) < LANES // 2
 
 
-def gate_kernel(query_ref, key_ref, value_ref, out_ref, pair_ref):
-    mixed = key_ref[...].astype(jnp.float32) * value_ref[...].astype(jnp.float32)
-    gated = out_ref[...].astype(jnp.float32) * query_ref[...].astype(jnp.float32)
-    left = left_mask(mixed.shape)
-    pair_ref[0] = jnp.where(left, mixed, pltpu.roll(gated, LANES // 2, 1))
-    pair_ref[1] = jnp.where(left, pltpu.roll(mixed, LANES // 2, 1), gated)
-
-
-def finish_kernel(pair_ref, query_ref, key_ref, value_ref, out_ref, skip_ref, gq_ref, gk_ref, gv_ref):
-    query_f = query_ref[...].astype(jnp.float32)
-    key_f = key_ref[...].astype(jnp.float32)
-    value_f = value_ref[...].astype(jnp.float32)
-    out_f = out_ref[...].astype(jnp.float32)
-    first, second = pair_ref[0], pair_ref[1]
-    left = left_mask(first.shape)
-    skip = skip_ref[...]
-    conv = jnp.where(left, first, pltpu.roll(second, LANES // 2, 1)) + skip * (key_f * value_f)
-    back = jnp.where(left, pltpu.roll(first, LANES // 2, 1), second) + skip * (out_f * query_f)
-    gq_ref[...] = (out_f * conv).astype(jnp.bfloat16)
-    gk_ref[...] = (back * value_f).astype(jnp.bfloat16)
-    gv_ref[...] = (back * key_f).astype(jnp.bfloat16)
+def far_first(seq_count, ch_count):
+    steps = sorted(range(seq_count), key=lambda step: abs(2 * step - seq_count))
+    return [(step, turn) for step in steps for turn in range(ch_count) if step or turn]
+
+
+def greet(seq_count, ch_count, me_seq, me_ch):
+    barrier = pltpu.get_barrier_semaphore()
+    partners = far_first(seq_count, ch_count)
+    for step, turn in partners:
+        pl.semaphore_signal(barrier, inc=1, device_id=partner_of(step, turn, seq_count, ch_count, me_seq, me_ch), device_id_type=pl.DeviceIdType.MESH)
+    pl.semaphore_wait(barrier, len(partners))
+
+
+def partner_of(step, turn, seq_count, ch_count, me_seq, me_ch):
+    return {"seq": lax.rem(me_seq + step, seq_count), "ch": lax.rem(me_ch + turn, ch_count)}
+
+
+def exchange(sends, seq_count, ch_count, me_seq, me_ch):
+    copies = []
+    for step, turn in far_first(seq_count, ch_count):
+        partner = partner_of(step, turn, seq_count, ch_count, me_seq, me_ch)
+        for source, target, send_sem, recv_sem, same_ch in sends:
+            if same_ch and turn:
+                continue
+            if same_ch:
+                give, take, slot = partner["seq"], me_seq, step
+            else:
+                give, take, slot = partner["ch"] * seq_count + partner["seq"], me_ch * seq_count + me_seq, step * ch_count + turn
+            copy = pltpu.make_async_remote_copy(
+                src_ref=source.at[give],
+                dst_ref=target.at[take],
+                send_sem=send_sem.at[slot],
+                recv_sem=recv_sem.at[slot],
+                device_id=partner,
+                device_id_type=pl.DeviceIdType.MESH,
+            )
+            copy.start()
+            copies.append(copy)
+    return copies
+
+
+def gate_kernel(seq_count, ch_count, query_ref, key_ref, value_ref, out_ref, filter_ref, pair_ref, send, recv, send_sem, recv_sem):
+    me_seq, me_ch = lax.axis_index("seq"), lax.axis_index("ch")
+    tokens = key_ref.shape[0]
+    share = tokens // ch_count
+    scale = (seq_count * tokens) ** -0.5
+    half_lanes = LANES // 2
+
+    def prepare(group, carry):
+        lanes = pl.ds(pl.multiple_of(group * LANES, LANES), LANES)
+        mixed = key_ref[:, lanes].astype(jnp.float32) * value_ref[:, lanes].astype(jnp.float32)
+        gated = out_ref[:, lanes].astype(jnp.float32) * query_ref[:, lanes].astype(jnp.float32)
+        left = left_mask(mixed.shape)
+        send[2 * group, :tokens, :] = jnp.where(left, mixed, pltpu.roll(gated, half_lanes, 1))
+        send[2 * group + 1, :tokens, :] = jnp.where(left, pltpu.roll(mixed, half_lanes, 1), gated)
+        rows = pl.ds(pl.multiple_of(me_ch * share, share), share)
+        taps = filter_ref[rows, lanes].astype(jnp.float32) * scale
+        top, bottom = taps[:share // 2], taps[share // 2:]
+        left = left_mask(top.shape)
+        send[2 * group, tokens:, :] = jnp.where(left, top, pltpu.roll(bottom, half_lanes, 1))
+        send[2 * group + 1, tokens:, :] = jnp.where(left, pltpu.roll(top, half_lanes, 1), bottom)
+        return carry
+
+    lax.fori_loop(0, seq_count, prepare, 0)
+    greet(seq_count, ch_count, me_seq, me_ch)
+    copies = exchange([(send, recv, send_sem, recv_sem, False)], seq_count, ch_count, me_seq, me_ch)
+    mine = me_ch * seq_count + me_seq
+    recv[mine] = send[mine]
+    for copy in copies:
+        copy.wait()
+
+    def hand_over(owner, carry):
+        pair_ref[owner] = recv[owner]
+        return carry
+
+    lax.fori_loop(0, seq_count * ch_count, hand_over, 0)
+
+
+def left_mask(shape):
+    return lax.broadcasted_iota(jnp.int32, shape, 1) < LANES // 2
+
+
+def finish_kernel(seq_count, ch_count, pair_ref, corr_ref, query_ref, key_ref, value_ref, out_ref, skip_ref, gq_ref, gk_ref, gv_ref, gf_ref, recv, corr_recv, send_sem, recv_sem, corr_send_sem, corr_recv_sem):
+    me_seq, me_ch = lax.axis_index("seq"), lax.axis_index("ch")
+    half_lanes = LANES // 2
+    half_tokens = key_ref.shape[0] // 2
+    greet(seq_count, ch_count, me_seq, me_ch)
+    copies = exchange(
+        [(pair_ref, recv, send_sem, recv_sem, False), (corr_ref, corr_recv, corr_send_sem, corr_recv_sem, True)],
+        seq_count, ch_count, me_seq, me_ch)
+    mine = me_ch * seq_count + me_seq
+    recv[mine] = pair_ref[mine]
+    corr_recv[me_seq] = corr_ref[me_seq]
+    for copy in copies:
+        copy.wait()
+
+    def finish(group, carry):
+        lanes = pl.ds(pl.multiple_of(group * LANES, LANES), LANES)
+        query_f = query_ref[:, lanes].astype(jnp.float32)
+        key_f = key_ref[:, lanes].astype(jnp.float32)
+        value_f = value_ref[:, lanes].astype(jnp.float32)
+        out_f = out_ref[:, lanes].astype(jnp.float32)
+        first, second = recv[2 * group], recv[2 * group + 1]
+        left = left_mask(first.shape)
+        skip = skip_ref[:, lanes]
+        conv = jnp.where(left, first, pltpu.roll(second, half_lanes, 1)) + skip * (key_f * value_f)
+        back = jnp.where(left, pltpu.roll(first, half_lanes, 1), second) + skip * (out_f * query_f)
+        gq_ref[:, lanes] = (out_f * conv).astype(jnp.bfloat16)
+        gk_ref[:, lanes] = (back * value_f).astype(jnp.bfloat16)
+        gv_ref[:, lanes] = (back * key_f).astype(jnp.bfloat16)
+        return carry
+
+    lax.fori_loop(0, seq_count, finish, 0)
+
+    def finish_corr(group, carry):
+        lanes = pl.ds(pl.multiple_of(group * LANES, LANES), LANES)
+        first, second = corr_recv[2 * group], corr_recv[2 * group + 1]
+        left = left_mask(first.shape)
+        gf_ref[:half_tokens, lanes] = jnp.where(left, first, pltpu.roll(second, half_lanes, 1))
+        gf_ref[half_tokens:, lanes] = jnp.where(left, pltpu.roll(first, half_lanes, 1), second)
+        return carry
+
+    lax.fori_loop(0, seq_count // 2, finish_corr, 0)
 
 
 def tables(seq_count, tokens):
@@ -342,27 +445,23 @@
     seq_count, ch_count = lax.axis_size("seq"), lax.axis_size("ch")
     owners = seq_count * ch_count
     _, tokens, channels = key_input.shape
-    length = seq_count * tokens
-    width = channels // owners
-    groups = channels // LANES
-    block = pl.BlockSpec((None, tokens, LANES), lambda i: (0, 0, i))
-    pair_block = pl.BlockSpec((2, tokens, LANES), lambda i: (i, 0, 0))
-    params = pltpu.CompilerParams(vmem_limit_bytes=VMEM_LIMIT)
+    rows = tokens + tokens // (2 * ch_count)
+    vmem = pl.BlockSpec(memory_space=pltpu.VMEM)
+    signals = (query_gate[0], key_input[0], value_input[0], grad_output[0])
     pair = pl.pallas_call(
-        gate_kernel,
-        grid=(groups,),
-        in_specs=[block] * 4,
-        out_specs=pair_block,
-        out_shape=jax.ShapeDtypeStruct((owners, tokens, LANES), jnp.float32),
+        lambda *refs: gate_kernel(seq_count, ch_count, *refs),
+        in_specs=[vmem] * 5,
+        out_specs=vmem,
+        out_shape=jax.ShapeDtypeStruct((owners, rows, LANES), jnp.float32),
+        scratch_shapes=[
+            pltpu.VMEM((owners, rows, LANES), jnp.float32),
+            pltpu.VMEM((owners, rows, LANES), jnp.float32),
+            pltpu.SemaphoreType.DMA((owners,)),
+            pltpu.SemaphoreType.DMA((owners,)),
+        ],
+        compiler_params=pltpu.CompilerParams(vmem_limit_bytes=VMEM_LIMIT, collective_id=0, has_side_effects=True),
         name="gate",
-    )(query_gate, key_input, value_input, grad_output)
-    mine = lax.axis_index("ch") * (channels // ch_count)
-    taps = lax.dynamic_slice_in_dim(filter_raw, mine, channels // ch_count, axis=1)
-    taps = taps.astype(jnp.float32) * length ** (-0.5)
-    taps = taps.reshape(2, tokens // 2, seq_count, width).transpose(2, 1, 0, 3)
-    taps = taps.reshape(seq_count, tokens // 2, LANES)
-    pair = lax.all_to_all(pair, ("ch", "seq"), split_axis=0, concat_axis=0, tiled=True)
-    taps = lax.all_to_all(taps, "seq", split_axis=0, concat_axis=0, tiled=True)
+    )(*signals, filter_raw)
     pair, corr = pl.pallas_call(
         lambda *refs: fft_kernel(seq_count, tokens, *refs),
         out_shape=(
@@ -374,21 +473,27 @@
             pltpu.VMEM((seq_count, tokens, LANES), jnp.float32),
             pltpu.VMEM((seq_count, tokens, LANES), jnp.float32),
         ],
-        compiler_params=params,
+        compiler_params=pltpu.CompilerParams(vmem_limit_bytes=VMEM_LIMIT),
         name="convolve",
-    )(pair.reshape(ch_count, seq_count, tokens, LANES), taps, *tables(seq_count, tokens))
-    pair = lax.all_to_all(pair.reshape(owners, tokens, LANES), ("ch", "seq"), split_axis=0, concat_axis=0, tiled=True)
-    corr = lax.all_to_all(corr, "seq", split_axis=0, concat_axis=0, tiled=True)
+    )(pair.reshape(ch_count, seq_count, rows, LANES), *tables(seq_count, tokens))
     grads = pl.pallas_call(
-        finish_kernel,
-        grid=(groups,),
-        in_specs=[pair_block] + [block] * 4 + [pl.BlockSpec((1, LANES), lambda i: (0, i))],
-        out_specs=[block] * 3,
-        out_shape=[jax.ShapeDtypeStruct(key_input.shape, jnp.bfloat16)] * 3,
+        lambda *refs: finish_kernel(seq_count, ch_count, *refs),
+        in_specs=[vmem] * 7,
+        out_specs=[vmem] * 4,
+        out_shape=[jax.ShapeDtypeStruct((tokens, channels), jnp.bfloat16)] * 3
+        + [jax.ShapeDtypeStruct((tokens, channels // ch_count), jnp.float32)],
+        scratch_shapes=[
+            pltpu.VMEM((owners, tokens, LANES), jnp.float32),
+            pltpu.VMEM((seq_count, tokens // 2, LANES), jnp.float32),
+            pltpu.SemaphoreType.DMA((owners,)),
+            pltpu.SemaphoreType.DMA((owners,)),
+            pltpu.SemaphoreType.DMA((seq_count,)),
+            pltpu.SemaphoreType.DMA((seq_count,)),
+        ],
+        compiler_params=pltpu.CompilerParams(vmem_limit_bytes=VMEM_LIMIT, collective_id=1, has_side_effects=True),
         name="finish",
-    )(pair, query_gate, key_input, value_input, grad_output, skip_gain[None])
-    corr = corr.reshape(seq_count, tokens // 2, 2, width).transpose(2, 1, 0, 3)
-    return (*grads, corr.reshape(tokens, seq_count * width))
+    )(pair.reshape(owners, tokens, LANES), corr, *signals, skip_gain[None])
+    return (grads[0][None], grads[1][None], grads[2][None], grads[3])
 
 
 def solution(mesh):

time: 190 us -> 168 us (0.88)
  the two profiles are of different devices: /device:TPU:0 before, /device:TPU:16 now
where the time goes in v1:
time: 168 us
  Pallas kernels  160 us (95%)
  local copies, waits for them, and re-layouts  7.45 us (4%)
    pallas_call x1, Pallas kernels, fast_shards(): pl.pallas_call(lambda *refs: finish_kernel(seq_count, ch_count, *refs), i...  68.4 us
    pallas_call x1, Pallas kernels, fast_shards(): pl.pallas_call(lambda *refs: gate_kernel(seq_count, ch_count, *refs), in_...  68 us
    pallas_call x1, Pallas kernels, fast_shards(): pl.pallas_call(lambda *refs: fft_kernel(seq_count, tokens, *refs), out_sh...  23.1 us
    unnamed x10, local copies, waits for them, and re-layouts  5.45 us

profile of v1, /device:TPU:16, one launch (start us, length us, event | category | flops | bytes accessed | tf_op | source)
XLA Modules:
  0.0 167.6 jit_solution(15086551128607811354)
XLA Ops:
  0.6 0.0 copy-start.2
  0.6 68.0 %gate.1 = f32[32,160,128]{2,1,0:T(8,128)} custom-call(bf16[128,2048]{1,0:T(8,128)(2,1)} %bitcast.11, bf16[128,2048]{1,0:T(8,128)(2,1)} %bitcast.13, bf16[128,2048]{1,0:T(8,128)(2,1)} %bitcast.15, bf16[128,2048]{1,0:T(8,128)(2,1)} %bitcast.17, bf16[128,2048]{1,0:T(8,128)(2,1)} %refs_4_.1), custom_call_target="tpu_custom_call" | custom-call | tf_op jit(solution)/shard_map/gate/pallas_call | solution.py:451
  68.7 0.0 copy-done.2
  68.7 2.0 %broadcast_in_dim.18.refs_3_ = f32[17,2,128,128]{3,2,1,0:T(8,128)} broadcast(f32[17,2,128]{2,1,0:T(2,128)S(1)} %copy-done.2), dimensions={0,1,2} | broadcast | bytes 2245632 | tf_op jit(solution)/shard_map/broadcast_in_dim | solution.py:440
  70.7 23.1 %convolve.1 = (f32[2,16,128,128]{3,2,1,0:T(8,128)}, f32[16,64,128]{2,1,0:T(8,128)}) custom-call(f32[2,16,160,128]{3,2,1,0:T(8,128)} %bitcast.10, bf16[2,256,256]{2,1,0:T(8,128)(2,1)} %constant.19.refs_1_, bf16[2,256,256]{2,1,0:T(8,128)(2,1)} %constant.26.refs_2_, f32[17,2,128,128]{3,2,1,0:T(8,128)} %broadcast_in_dim.18.refs_3_), custom_call_target="tpu_custom_call" | custom-call | tf_op jit(solution)/shard_map/convolve/pallas_call | solution.py:465
  93.7 68.4 %finish.1 = (bf16[128,2048]{1,0:T(8,128)(2,1)}, bf16[128,2048]{1,0:T(8,128)(2,1)}, bf16[128,2048]{1,0:T(8,128)(2,1)}, f32[128,1024]{1,0:T(8,128)}) custom-call(f32[32,128,128]{2,1,0:T(8,128)} %bitcast.19, f32[16,64,128]{2,1,0:T(8,128)} %get-tuple-element.11.refs_1_, bf16[128,2048]{1,0:T(8,128)(2,1)} %bitcast.12, bf16[128,2048]{1,0:T(8,128)(2,1)} %bitcast.14, ...), custom_call_target="tpu_custom_call" | custom-call | tf_op jit(solution)/shard_map/finish/pallas_call | solution.py:479
  162.2 0.0 copy-start.1
  162.2 0.0 copy-start
  162.2 2.0 %copy.17 = bf16[1,128,2048]{2,1,0:T(8,128)(2,1)} copy(bf16[1,128,2048]{2,1,0:T(8,128)(2,1)} %bitcast.22) | data formatting | bytes 1048576
  164.2 1.9 %copy.18 = bf16[1,128,2048]{2,1,0:T(8,128)(2,1)} copy(bf16[1,128,2048]{2,1,0:T(8,128)(2,1)} %bitcast.21) | data formatting | bytes 1048576
  166.0 0.0 copy-done.1
  166.0 0.8 copy.19
  166.8 0.0 copy-done
  166.8 0.8 copy.20
Async XLA Ops:
  0.6 68.0 %copy-start.2 = (f32[17,2,128]{2,1,0:T(2,128)S(1)}, f32[17,2,128]{2,1,0:T(2,128)}, u32[]{:S(2)}) copy-start(f32[17,2,128]{2,1,0:T(2,128)} %constant.6.clone) | copy-start | bytes 52228
  162.2 3.9 %copy-start.1 = (bf16[128,2048]{1,0:T(8,128)(2,1)S(1)}, bf16[128,2048]{1,0:T(8,128)(2,1)}, u32[]{:S(2)}) copy-start(bf16[128,2048]{1,0:T(8,128)(2,1)} %get-tuple-element.14) | copy-start | bytes 1572868
  162.2 4.7 %copy-start = (f32[128,1024]{1,0:T(8,128)S(1)}, f32[128,1024]{1,0:T(8,128)}, u32[]{:S(2)}) copy-start(f32[128,1024]{1,0:T(8,128)} %get-tuple-element.23) | copy-start | bytes 1572868
